TPU v7x, 32 devices: a whole 2x2x4 slice. The times are simulated.
32 devices in a mesh: gx: 4 (over y, core), gy: 2 (over x), var: 4 (over z).
Axes of the slice: x: 2, y: 2, z: 4, core: 2. Of those that a mesh axis runs over, the one named last changes fastest.
Arguments:
- field: float32 [4, 32, 256, 256], P('var', None, 'gx', 'gy'), may hold values from -12 to 12
- drive: float32 [4, 32, 40, 40], P('var'), may hold values from -1 to 1
- keep_count: int32 [32], replicated, may hold values from 20 to 79, as said below
- level_class: int32 [32], replicated, may hold values from 0 to 7
- height_table: float32 [8], replicated, may hold values from 0.2 to 1
Outputs:
- nudged: float32 [4, 32, 256, 256], P('var', None, 'gx', 'gy')
Inputs may be any that keep to these rules, and one draw needn't show every extreme that they name: `keep_count`: some level in every draw has the count 2 * 40 - 1, which keeps all 40 x 40 modes.
All inputs are finite; a program needn't handle non-finite values.
Results may differ from a plain program's by a relative error of at most 0.0001.
Values sent between devices are 32-bit elements; how exact they have to be, the bound alone decides.
No kernel may reach another device: no remote copies, remote signals or barrier semaphores. Data moves between devices by JAX's collectives and lax.ppermute only.
A program may use at most 64 MiB of HBM per device.

v0:
```python
import math
import jax
import jax.numpy as jnp
from jax import lax
from jax.sharding import PartitionSpec as P

NVAR = 4
KM = 40
HTAB = 8
energy_weights = (1.0, 1.0, 2.0, 3.0)
strength_top = 0.5
epsilon = 1e-06


def cosine_table(first, count, total, modes):
    cells = first + jnp.arange(count, dtype=jnp.int32)
    waves = jnp.arange(modes, dtype=jnp.int32)
    phase = waves[None, :] * (2 * cells[:, None] + 1) % (4 * total)
    values = jnp.cos(jnp.pi * phase.astype(jnp.float32) / (2.0 * total))
    factor = jnp.where(waves == 0, 1.0, math.sqrt(2.0)).astype(jnp.float32)
    return values * factor[None, :]


def settle(coeff, drive_block, mask, weight):
    delta = mask * (drive_block - coeff)
    gap = weight * jnp.sum(delta * delta)
    model = weight * jnp.sum(mask * coeff * coeff)
    gap, model = lax.psum((gap, model), "var")
    return (delta, gap, model)


def per_device(field, drive, keep_count, level_class, height_table):
    high = lax.Precision.HIGHEST
    block = field[0]
    drive_block = drive[0]
    levels, rows, columns = block.shape
    total_x = rows * lax.axis_size("gx")
    total_y = columns * lax.axis_size("gy")
    table_x = cosine_table(lax.axis_index("gx") * rows, rows, total_x, KM)
    table_y = cosine_table(lax.axis_index("gy") * columns, columns, total_y, KM)
    waves = jnp.arange(KM, dtype=jnp.int32)
    mask = ((waves[:, None] + waves[None, :])[None, :, :] < keep_count[:, None, None]).astype(
        jnp.float32
    )
    onehot = (level_class[:, None] == jnp.arange(HTAB, dtype=jnp.int32)[None, :]).astype(
        jnp.float32
    )
    lift = jnp.dot(onehot, height_table, precision=high)
    variable = lax.axis_index("var")
    weight = jnp.sum(
        jnp.where(
            jnp.arange(NVAR, dtype=jnp.int32) == variable,
            jnp.array(energy_weights, jnp.float32),
            0.0,
        )
    )
    half = jnp.einsum("lij,im->lmj", block, table_x, precision=high)
    partial_value = jnp.einsum("lmj,jn->lmn", half, table_y, precision=high) / float(
        total_x * total_y
    )
    flat = partial_value.reshape(-1)
    summed = lax.psum(flat, ("gx", "gy"))
    delta, gap, model = settle(summed.reshape(levels, KM, KM), drive_block, mask, weight)
    strength = strength_top * gap / (gap + model + epsilon)
    back = jnp.einsum("lmn,jn->lmj", delta, table_y, precision=high)
    increment = jnp.einsum("lmj,im->lij", back, table_x, precision=high)
    nudged = block + strength * lift[:, None, None] * increment
    return nudged[None]


def solution(mesh):
    return jax.shard_map(
        per_device,
        mesh=mesh,
        in_specs=(P("var", None, "gx", "gy"), P("var", None, None, None), P(), P(), P()),
        out_specs=P("var", None, "gx", "gy"),
        check_vma=False,
    )
```

profile of v0, /device:TPU:0, one launch (start us, length us, event | category | flops | bytes accessed | tf_op | source)
XLA Modules:
  0.0 97.3 jit_solution(9964165065591714958)
XLA Ops:
  6.5 0.0 copy-start
  6.5 0.0 all-reduce.3.cloned.1.call-start
  6.6 2.0 %convolution_bitcast_fusion = f32[32,40,128]{2,1,0:T(8,128)S(1)} fusion(f32[1,32,64,128]{3,2,1,0:T(8,128)} %param.6, f32[40]{0:T(128)S(1)} %compare_select_fusion, s32[64]{0:T(128)S(1)} %multiply_add_fusion.1), kind=kOutput, calls=%fused_computation.5 | convolution fusion | flops 125867520 | bytes 1704352 | tf_op jit(solution)/shard_map/lij,im->lmj/dot_general | solution.py:57
  8.6 0.7 convolution_multiply_fusion.1
  9.3 1.1 %reshape.46 = f32[51200]{0:T(1024)} reshape(f32[32,40,40]{2,1,0:T(8,128)S(1)} %convolution_multiply_fusion.1) | data formatting | bytes 409600 | tf_op jit(solution)/shard_map/reshape | solution.py:61
  10.5 0.0 all-reduce.3.cloned.1.call-update
  10.5 0.0 copy-start.3
  10.5 0.6 copy-done.3
  11.2 0.0 copy-start.5
  11.2 0.2 broadcast_compare_fusion
  11.3 0.0 copy-start.2
  11.3 0.5 lt.34
  11.9 0.0 copy-done.5
  11.9 0.6 fusion.56
  12.5 53.3 %all-reduce.3.cloned.1.call-done = f32[51200]{0:T(1024)} async-done(((f32[51200]{0:T(1024)}), f32[51200]{0:T(1024)}) %all-reduce.3.cloned.1.call-update) | async-done | bytes 204816 | tf_op jit(solution)/shard_map/psum | solution.py:62
  65.8 1.6 %fusion.6 = f32[]{:T(128)} fusion(f32[51200]{0:T(1024)} %all-reduce.3.cloned.1.call-done, pred[51200]{0:T(1024)(128)(4,1)S(1)} %lt.34), kind=kLoop, calls=%fused_computation.14 | loop fusion | flops 153599 | bytes 256004 | tf_op jit(solution)/shard_map/reduce_sum | solution.py:27
  68.7 1.4 %reshape.47 = f32[32,40,40]{2,1,0:T(8,128)S(1)} reshape(f32[51200]{0:T(1024)} %all-reduce.3.cloned.1.call-done) | data formatting | bytes 409600 | tf_op jit(solution)/shard_map/reshape | solution.py:63
  70.1 0.0 copy-done.2
  70.1 1.0 multiply_reduce_fusion
  71.0 0.0 copy-start.1
  72.4 0.8 fusion.7
  73.2 12.3 %all-reduce = (f32[]{:T(128)}, f32[]{:T(128)}) all-reduce(f32[]{:T(128)S(6)} %mul.129, f32[]{:T(128)S(6)} %mul.132), channel_id=1, replica_groups=mesh['gx'=4,'gy'=2,'var'=4] {'var'}, use_global_device_ids=true, to_apply=%region_3.4 | all-reduce | flops 2 | bytes 16 | tf_op jit(solution)/shard_map/psum | solution.py:28
  87.5 0.0 copy-start.4
  87.5 0.0 copy-done
  87.5 0.6 copy-done.4
  88.1 0.2 fusion.3
  88.3 0.0 copy-done.1
  88.3 2.2 %fusion.2 = f32[1,32,64,128]{3,2,1,0:T(8,128)} fusion(f32[32,40,128]{2,1,0:T(8,128)S(1)} %fusion.7, f32[1,32,64,128]{3,2,1,0:T(8,128)S(1)} %copy-done.1, f32[32]{0:T(128)S(1)} %fusion.3, f32[40]{0:T(128)S(1)} %compare_select_fusion, s32[64]{0:T(128)S(1)} %multiply_add_fusion.1), kind=kOutput, calls=%fused_computation.3 | convolution fusion | flops 126391808 | bytes 2753056 | tf_op jit(solution)/shard_map/lmj,im->lij/dot_general | solution.py:66
  (4 shorter events, 0.0 us)
Async XLA Ops:
  6.5 81.0 %copy-start = (f32[8]{0:T(128)S(1)}, f32[8]{0:T(128)}, u32[]{:S(2)}) copy-start(f32[8]{0:T(128)} %param.10) | copy-start | bytes 100
  6.5 59.2 %all-reduce.3.cloned.1.call-start = ((), (), s32[]{:S(2)}) async-start(), calls=%async_computation | async-start | bytes 409600 | tf_op jit(solution)/shard_map/psum | solution.py:62
  10.5 0.7 copy-start.3
  11.2 0.7 copy-start.5
  11.3 58.7 %copy-start.2 = (f32[1,32,40,40]{3,2,1,0:T(8,128)S(1)}, f32[1,32,40,40]{3,2,1,0:T(8,128)}, u32[]{:S(2)}) copy-start(f32[1,32,40,40]{3,2,1,0:T(8,128)} %param.7) | copy-start | bytes 614404
  71.0 17.3 %copy-start.1 = (f32[1,32,64,128]{3,2,1,0:T(8,128)S(1)}, f32[1,32,64,128]{3,2,1,0:T(8,128)}, u32[]{:S(2)}) copy-start(f32[1,32,64,128]{3,2,1,0:T(8,128)} %param.6) | copy-start | bytes 3145732
  87.5 0.7 copy-start.4
Sparse Core Ops, SparseCore 0:
  10.6 55.1 all-reduce.2
where the time goes:
time: 97.6 us; the launch traced here: 97.3 us
  waiting for transfers between devices  53.3 us (55%)
  between operations  18.2 us (19%)
  blocking collectives  12.3 us (13%)
  matrix products  5.85 us (6%)
  local copies, waits for them, and re-layouts  4.31 us (4%)
  other arithmetic  3.37 us (3%)
    psum x1, waiting for transfers between devices, per_device(): summed = lax.psum(flat, ('gx', 'gy'))  53.3 us
    psum x1, blocking collectives, settle(): gap, model = lax.psum((gap, model), 'var')  12.3 us
    dot_general x1, matrix products, per_device(): increment = jnp.einsum('lmj,im->lij', back, table_x, precision=high)  2.15 us
    dot_general x1, matrix products, per_device(): half = jnp.einsum('lij,im->lmj', block, table_x, precision=high)  2 us
  transfers between devices with their start and end apart: 1, of which 1 were waited for; matrix products, arithmetic and copies ran while one was open for 1% of the time, Pallas kernels for 0%

commit v1 on v0

--- a/solution.py
+++ b/solution.py
@@ -59,7 +59,8 @@
         total_x * total_y
     )
     flat = partial_value.reshape(-1)
-    summed = lax.psum(flat, ("gx", "gy"))
+    shards = lax.all_gather(flat, ("gx", "gy"), axis=0, tiled=False)
+    summed = shards.sum(axis=0)
     delta, gap, model = settle(summed.reshape(levels, KM, KM), drive_block, mask, weight)
     strength = strength_top * gap / (gap + model + epsilon)
     back = jnp.einsum("lmn,jn->lmj", delta, table_y, precision=high)

time: 97.6 us -> 70.5 us (0.72)
  waiting for transfers between devices: 53.3 us -> 28.1 us
  local copies, waits for them, and re-layouts: 4.31 us -> 1.73 us
    psum x1 -> x0, waiting for transfers between devices: 53.3 us -> none  [per_device(): summed = lax.psum(flat, ('gx', 'gy'))]
    all_gather x0 -> x1, waiting for transfers between devices: none -> 28.1 us  [per_device(): shards = lax.all_gather(flat, ('gx', 'gy'), axis=0, tiled=False)]
    reduce_sum x1, other arithmetic: 0.97 us -> 2.61 us  [per_device(): summed = shards.sum(axis=0)]
    reshape x1 -> x0, local copies, waits for them, and re-layouts: 1.15 us -> none  [per_device(): flat = partial_value.reshape(-1)]
where the time goes in v1:
time: 70.5 us; the launch traced here: 70.2 us
  waiting for transfers between devices  28.1 us (40%)
  between operations  18 us (26%)
  blocking collectives  12.3 us (17%)
  matrix products  5.86 us (8%)
  other arithmetic  4.26 us (6%)
  local copies, waits for them, and re-layouts  1.73 us (2%)
    all_gather x1, waiting for transfers between devices, per_device(): shards = lax.all_gather(flat, ('gx', 'gy'), axis=0, tiled=False)  28.1 us
    psum x1, blocking collectives, settle(): gap, model = lax.psum((gap, model), 'var')  12.3 us
    reduce_sum x1, other arithmetic, per_device(): summed = shards.sum(axis=0)  2.61 us
    dot_general x1, matrix products, per_device(): increment = jnp.einsum('lmj,im->lij', back, table_x, precision=high)  2.16 us
    dot_general x1, matrix products, per_device(): half = jnp.einsum('lij,im->lmj', block, table_x, precision=high)  2 us
  transfers between devices with their start and end apart: 1, of which 1 were waited for; matrix products, arithmetic and copies ran while one was open for 1% of the time, Pallas kernels for 0%

profile of v1, /device:TPU:0, one launch (start us, length us, event | category | flops | bytes accessed | tf_op | source)
XLA Modules:
  0.0 70.2 jit_solution(18307409709534928863)
XLA Ops:
  6.5 0.0 copy-start
  6.5 0.0 all-gather.3.cloned.1.call-start
  6.6 0.0 copy-start.5
  6.6 2.0 %convolution_bitcast_fusion = f32[32,40,128]{2,1,0:T(8,128)S(1)} fusion(f32[1,32,64,128]{3,2,1,0:T(8,128)} %param.6, f32[40]{0:T(128)S(1)} %compare_select_fusion.2, s32[64]{0:T(128)S(1)} %multiply_add_fusion.1), kind=kOutput, calls=%fused_computation.5 | convolution fusion | flops 125867520 | bytes 1704352 | tf_op jit(solution)/shard_map/lij,im->lmj/dot_general | solution.py:57
  8.6 0.7 %convolution_multiply_fusion.1 = f32[32,40,40]{2,1,0:T(8,128)S(1)} fusion(f32[32,40,128]{2,1,0:T(8,128)S(1)} %convolution_bitcast_fusion, f32[40]{0:T(128)S(1)} %compare_select_fusion.2, s32[128]{0:T(128)S(1)} %multiply_add_fusion), kind=kOutput, calls=%fused_computation.4 | convolution fusion | flops 78771200 | bytes 860832 | tf_op jit(solution)/shard_map/lmj,jn->lmn/dot_general | solution.py:58
  9.3 1.2 %reshape.47 = f32[1,1,51200]{2,1,0:T(1,128)} reshape(f32[32,40,40]{2,1,0:T(8,128)S(1)} %convolution_multiply_fusion.1) | data formatting | bytes 409600
  10.6 0.0 copy-start.2
  10.6 0.0 copy-start.3
  10.6 0.0 all-gather.3.cloned.1.call-update
  10.6 0.0 copy-done.5
  10.6 0.6 fusion.54
  11.2 28.1 %all-gather.3.cloned.1.call-done = f32[8,1,51200]{2,1,0:T(1,128)} async-done(((f32[1,1,51200]{2,1,0:T(1,128)}), f32[8,1,51200]{2,1,0:T(1,128)}) %all-gather.3.cloned.1.call-update) | async-done | bytes 1638416 | tf_op jit(solution)/shard_map/all_gather | solution.py:62
  39.3 2.6 %reduce_sum.37 = f32[51200]{0:T(1024)S(1)} reduce(f32[8,1,51200]{2,1,0:T(1,128)} %all-gather.3.cloned.1.call-done, f32[]{:T(128)} %constant.30.clone.1), dimensions={0,1}, to_apply=%region_1.2 | reduce | flops 358400 | bytes 1843204 | tf_op jit(solution)/shard_map/reduce_sum | solution.py:63
  42.0 0.5 reshape.46
  42.4 0.0 copy-done.2
  42.4 0.0 copy-done.3
  42.4 0.0 copy-start.4
  42.4 0.0 copy-start.1
  42.5 1.1 %fusion.5 = (f32[]{:T(128)}, f32[]{:T(128)}) fusion(f32[32,40,40]{2,1,0:T(8,128)S(1)} %reshape.46, s32[40,40]{1,0:T(8,128)S(1)} %iota_add_fusion, s32[32]{0:T(128)S(1)} %copy-done.3, f32[1,32,40,40]{3,2,1,0:T(8,128)S(1)} %copy-done.2), kind=kLoop, calls=%fused_computation.11 | loop fusion | flops 409598 | bytes 416136 | tf_op jit(solution)/shard_map/reduce_sum | solution.py:27
  45.9 0.8 %fusion.6 = f32[32,40,128]{2,1,0:T(8,128)S(1)} fusion(f32[32,40,40]{2,1,0:T(8,128)S(1)} %reshape.46, f32[1,32,40,40]{3,2,1,0:T(8,128)S(1)} %copy-done.2, s32[40,40]{1,0:T(8,128)S(1)} %iota_add_fusion, s32[32]{0:T(128)S(1)} %copy-done.3, f32[40]{0:T(128)S(1)} %compare_select_fusion.2, s32[128]{0:T(128)S(1)} %multiply_add_fusion), kind=kOutput, calls=%fused_computation.14 | convolution fusion | flops 78873600 | bytes 1072160 | tf_op jit(solution)/shard_map/lmn,jn->lmj/dot_general | solution.py:66
  46.7 12.3 %all-reduce = (f32[]{:T(128)}, f32[]{:T(128)}) all-reduce(f32[]{:T(128)S(6)} %mul.132, f32[]{:T(128)S(6)} %mul.135), channel_id=1, replica_groups=mesh['gx'=4,'gy'=2,'var'=4] {'var'}, use_global_device_ids=true, to_apply=%region_3.4 | all-reduce | flops 2 | bytes 16 | tf_op jit(solution)/shard_map/psum | solution.py:28
  61.0 0.0 copy-done
  61.0 0.0 copy-done.4
  61.0 0.2 fusion.3
  61.2 0.0 copy-done.1
  61.2 2.2 %fusion.2 = f32[1,32,64,128]{3,2,1,0:T(8,128)} fusion(f32[32,40,128]{2,1,0:T(8,128)S(1)} %fusion.6, f32[1,32,64,128]{3,2,1,0:T(8,128)S(1)} %copy-done.1, f32[32]{0:T(128)S(1)} %fusion.3, f32[40]{0:T(128)S(1)} %compare_select_fusion.2, s32[64]{0:T(128)S(1)} %multiply_add_fusion.1), kind=kOutput, calls=%fused_computation.3 | convolution fusion | flops 126391808 | bytes 2753056 | tf_op jit(solution)/shard_map/lmj,im->lij/dot_general | solution.py:67
  (4 shorter events, 0.0 us)
Async XLA Ops:
  6.5 54.5 %copy-start = (f32[8]{0:T(128)S(1)}, f32[8]{0:T(128)}, u32[]{:S(2)}) copy-start(f32[8]{0:T(128)} %param.10) | copy-start | bytes 100
  6.5 32.8 %all-gather.3.cloned.1.call-start = ((), (), s32[]{:S(2)}) async-start(), calls=%async_computation | async-start | bytes 1843200 | tf_op jit(solution)/shard_map/all_gather | solution.py:62
  6.6 4.1 %copy-start.5 = (f32[4]{0:T(128)S(1)}, f32[4]{0:T(128)}, u32[]{:S(2)}) copy-start(f32[4]{0:T(128)} %constant.72.clone) | copy-start | bytes 52
  10.6 31.8 %copy-start.2 = (f32[1,32,40,40]{3,2,1,0:T(8,128)S(1)}, f32[1,32,40,40]{3,2,1,0:T(8,128)}, u32[]{:S(2)}) copy-start(f32[1,32,40,40]{3,2,1,0:T(8,128)} %param.7) | copy-start | bytes 614404
  10.6 31.8 %copy-start.3 = (s32[32]{0:T(128)S(1)}, s32[32]{0:T(128)}, u32[]{:S(2)}) copy-start(s32[32]{0:T(128)} %param.8) | copy-start | bytes 388
  42.4 18.6 %copy-start.4 = (s32[32]{0:T(128)S(1)}, s32[32]{0:T(128)}, u32[]{:S(2)}) copy-start(s32[32]{0:T(128)} %param.9) | copy-start | bytes 388
  42.4 18.8 %copy-start.1 = (f32[1,32,64,128]{3,2,1,0:T(8,128)S(1)}, f32[1,32,64,128]{3,2,1,0:T(8,128)}, u32[]{:S(2)}) copy-start(f32[1,32,64,128]{3,2,1,0:T(8,128)} %param.6) | copy-start | bytes 3145732
Sparse Core Ops, SparseCore 0:
  10.7 28.5 all-gather.2
